TPU v7x, 32 devices: a whole 2x2x4 slice. The times are simulated.
32 devices in a mesh: rows: 8 (over z, x), cols: 4 (over y, core).
Axes of the slice: x: 2, y: 2, z: 4, core: 2. Of those that a mesh axis runs over, the one named last changes fastest.
Arguments:
- basis: bfloat16 [65536, 512], P('rows', 'cols'), may hold values from -6 to 6
- lower: bfloat16 [256, 256, 256], P('rows'), may hold values from -0.375 to 0.375
- diag: bfloat16 [256, 256, 256], P('rows'), may hold values from -0.375 to 0.375
- upper: bfloat16 [256, 256, 256], P('rows'), may hold values from -0.375 to 0.375
- inverse: bfloat16 [256, 256, 256], P('rows'), may hold values from -0.375 to 0.375
Outputs:
- ortho: bfloat16 [65536, 512], P('rows', 'cols')
- projected: float32 [512, 512], P(None, 'cols')
All inputs are finite; a program needn't handle non-finite values.
Results may differ from a plain program's by a relative error of at most 0.0085.
Values may be sent and summed in bfloat16 or wider, within the bound.
A program may use at most 128 MiB of HBM per device.

v0:
```python
import jax
import jax.numpy as jnp
from jax import lax
from jax.sharding import PartitionSpec as P


def extended(block, sides, width):
    for axis, dim in sides:
        count = lax.axis_size(axis)
        forward = [(i, i + 1) for i in range(count - 1)]
        backward = [(target, source) for source, target in forward]
        low = lax.ppermute(
            lax.slice_in_dim(block, block.shape[dim] - width, None, axis=dim), axis, forward
        )
        high = lax.ppermute(lax.slice_in_dim(block, 0, width, axis=dim), axis, backward)
        block = jnp.concatenate([low, block, high], axis=dim)
    return block


def inner(left, right):
    return lax.dot_general(
        left, right, (((0,), (0,)), ((), ())), preferred_element_type=jnp.float32
    )


def apply_blocks(padded, lower, diag, upper, inverse):
    count = diag.shape[0]
    size = diag.shape[1]
    width = padded.shape[1]
    blocks = padded.reshape(count + 2, size, width)
    mixed = jnp.einsum("bij,bjc->bic", lower, blocks[:-2], preferred_element_type=jnp.float32)
    mixed = mixed + jnp.einsum(
        "bij,bjc->bic", diag, blocks[1:-1], preferred_element_type=jnp.float32
    )
    mixed = mixed + jnp.einsum(
        "bij,bjc->bic", upper, blocks[2:], preferred_element_type=jnp.float32
    )
    mixed = mixed.astype(jnp.bfloat16)
    result = jnp.einsum("bij,bjc->bic", inverse, mixed, preferred_element_type=jnp.float32)
    return result.astype(jnp.bfloat16).reshape(count * size, width)


def inverse_upper(gram):
    factor = jnp.linalg.cholesky(gram)
    identity = jnp.eye(gram.shape[0], dtype=jnp.float32)
    linv = lax.linalg.triangular_solve(factor, identity, left_side=True, lower=True)
    return linv.T.astype(jnp.bfloat16)


def shards(basis, lower, diag, upper, inverse):
    size = diag.shape[1]
    width = basis.shape[1]

    def operate(field):
        padded = extended(field, (("rows", 0),), size)
        return apply_blocks(padded, lower, diag, upper, inverse)

    work = operate(basis)
    wide = lax.all_gather(work, "cols", axis=1, tiled=True)
    gram = lax.psum(inner(wide, wide), "rows")
    rinv = inverse_upper(gram)
    start = lax.axis_index("cols") * width
    ortho_all = jnp.dot(wide, rinv, preferred_element_type=jnp.float32).astype(jnp.bfloat16)
    ortho = lax.dynamic_slice_in_dim(ortho_all, start, width, 1)
    image = operate(ortho)
    projected = lax.psum(inner(ortho_all, image), "rows")
    return (ortho, projected)


def solution(mesh):
    in_specs = (
        P("rows", "cols"),
        P("rows", None, None),
        P("rows", None, None),
        P("rows", None, None),
        P("rows", None, None),
    )
    out_specs = (P("rows", "cols"), P(None, "cols"))
    return jax.shard_map(shards, mesh=mesh, in_specs=in_specs, out_specs=out_specs, check_vma=False)
```

profile of v0, /device:TPU:0, one launch (start us, length us, event | category | flops | bytes accessed | tf_op | source)
XLA Modules:
  0.0 457.5 jit_solution(3944854083608453380)
XLA Ops:
  9.4 5.5 %collective-permute-start = (bf16[256,128]{1,0:T(8,128)(2,1)S(1)}, bf16[256,128]{1,0:T(8,128)(2,1)S(1)}, u32[]{:S(2)}, u32[]{:S(2)}) collective-permute-start(bf16[256,128]{1,0:T(8,128)(2,1)S(1)} %get-tuple-element.27), channel_id=1, source_target_pairs={{0,4},{4,8},{8,12},{12,16},{16,20},{20,24},{24,28},{1,5},{5,9},{9,... | collective-permute-start | bytes 196616 | tf_op jit(solution)/shard_map/ppermute | solution.py:12
  14.9 6.5 %fusion.49 = f32[32,256,128]{1,2,0:T(8,128)} fusion(bf16[32,256,256]{2,1,0:T(8,128)(2,1)} %param.7, bf16[32,256,128]{2,1,0:T(8,128)(2,1)} %bitcast.98), kind=kOutput, calls=%fused_computation.97 | convolution fusion | flops 536870912 | bytes 10485760 | tf_op jit(solution)/shard_map/bij,bjc->bic/dot_general | solution.py:32
  21.7 1.9 copy-done.2
  23.6 3.5 fusion.48
  27.0 10.1 %convert_bitcast_fusion.1 = bf16[32,256,128]{1,2,0:T(8,128)(2,1)} fusion(bf16[32,256,256]{2,1,0:T(8,128)(2,1)} %param.9, f32[32,256,128]{1,2,0:T(8,128)} %fusion.49, f32[32,128,256]{2,1,0:T(8,128)} %fusion.48, bf16[32,256,128]{2,1,0:T(8,128)(2,1)S(1)} %bitcast.99, bf16[32,256,256]{2,1,0:T(8,128)(2,1)} %param.8), kind=kOutput, calls=%fused_computation.14 | convolution fusion | flops 1077936128 | bytes 20971520 | tf_op jit(solution)/shard_map/bij,bjc->bic/dot_general | solution.py:39
  37.1 4.0 copy.9
  41.2 61.1 %all-gather.2.cloned.1.call-done = bf16[8192,512]{1,0:T(8,128)(2,1)} async-done(((bf16[8192,128]{1,0:T(8,128)(2,1)}), bf16[8192,512]{1,0:T(8,128)(2,1)}) %all-gather.2.cloned.1.call-update) | async-done | bytes 8388624 | tf_op jit(solution)/shard_map/all_gather | solution.py:59
  102.4 11.3 %fusion.50 = f32[512,512]{0,1:T(8,128)} fusion(bf16[8192,512]{1,0:T(8,128)(2,1)} %all-gather.2.cloned.1.call-done), kind=kOutput, calls=%fused_computation.98 | convolution fusion | flops 4294967296 | bytes 9437184 | tf_op jit(solution)/shard_map/dot_general | solution.py:21
  114.8 77.2 %all-reduce.4.cloned.1.call-done = f32[512,512]{0,1:T(8,128)} async-done(((f32[512,512]{0,1:T(8,128)}), f32[512,512]{0,1:T(8,128)}) %all-reduce.4.cloned.1.call-update) | async-done | bytes 1048592 | tf_op jit(solution)/shard_map/psum | solution.py:60
  195.1 11.7 %cholesky.104 = f32[128,128]{1,0:T(8,128)S(1)} custom-call(f32[128,128]{1,0:T(8,128)S(1)} %cholesky.266), custom_call_target="Cholesky" | custom-call | tf_op jit(solution)/shard_map/jit(cholesky)/cholesky | solution.py:44
  206.8 9.8 %custom-call.30 = f32[1,128,128]{1,2,0:T(8,128)S(1)} custom-call(f32[1,128,128]{2,1,0:T(8,128)S(1)} %get-tuple-element.37), custom_call_target="InvertDiagBlocksLowerTriangular" | custom-call | tf_op jit(solution)/shard_map/jit(cholesky)/cholesky | solution.py:44
  217.4 11.7 %cholesky.217 = f32[128,128]{1,0:T(8,128)S(1)} custom-call(f32[128,128]{1,0:T(8,128)S(1)} %cholesky.270), custom_call_target="Cholesky" | custom-call | tf_op jit(solution)/shard_map/jit(cholesky)/cholesky | solution.py:44
  229.2 10.0 %custom-call.31 = f32[1,128,128]{1,2,0:T(8,128)S(1)} custom-call(f32[1,128,128]{2,1,0:T(8,128)S(1)} %get-tuple-element.34), custom_call_target="InvertDiagBlocksLowerTriangular" | custom-call | tf_op jit(solution)/shard_map/jit(cholesky)/cholesky | solution.py:44
  239.8 11.7 %cholesky.238 = f32[128,128]{1,0:T(8,128)S(1)} custom-call(f32[128,128]{1,0:T(8,128)S(1)} %cholesky.275), custom_call_target="Cholesky" | custom-call | tf_op jit(solution)/shard_map/jit(cholesky)/cholesky | solution.py:44
  252.3 9.8 %custom-call.32 = f32[1,128,128]{1,2,0:T(8,128)S(1)} custom-call(f32[1,128,128]{2,1,0:T(8,128)S(1)} %get-tuple-element.31), custom_call_target="InvertDiagBlocksLowerTriangular" | custom-call | tf_op jit(solution)/shard_map/jit(cholesky)/cholesky | solution.py:44
  262.7 11.7 %cholesky.255 = f32[128,128]{1,0:T(8,128)S(1)} custom-call(f32[128,128]{1,0:T(8,128)S(1)} %convolution_subtract_fusion.5), custom_call_target="Cholesky" | custom-call | tf_op jit(solution)/shard_map/jit(cholesky)/cholesky | solution.py:44
  278.9 10.8 %while.1 = (s32[]{:T(128)}, f32[512,512]{1,0:T(8,128)S(1)}, s32[4,2]{0,1:T(2,128)S(1)}, f32[4,128,128]{2,1,0:T(8,128)}, s32[]{:T(128)}) while((s32[]{:T(128)}, f32[512,512]{1,0:T(8,128)S(1)}, s32[4,2]{0,1:T(2,128)S(1)}, f32[4,128,128]{2,1,0:T(8,128)}, s32[]{:T(128)}) %tuple.38), condition=%wide.while_cond, body=%wide.while_body.sunk | while | flops 2 | bytes 132205 | solution.py:46
  279.6 2.0 bitcast_dynamic-update-slice_fusion.2
  282.3 2.0 bitcast_dynamic-update-slice_fusion.2
  285.0 2.0 bitcast_dynamic-update-slice_fusion.2
  287.7 2.1 bitcast_dynamic-update-slice_fusion.2
  289.7 40.1 %custom-call.33 = f32[4,128,128]{1,2,0:T(8,128)S(1)} custom-call(f32[4,128,128]{2,1,0:T(8,128)} %get-tuple-element.9), custom_call_target="InvertDiagBlocksLowerTriangular" | custom-call | tf_op jit(solution)/shard_map/triangular_solve | solution.py:46
  333.7 8.8 %convolution_convert_fusion = bf16[8192,512]{1,0:T(8,128)(2,1)S(1)} fusion(bf16[8192,512]{1,0:T(8,128)(2,1)} %all-gather.2.cloned.1.call-done, bf16[128,512]{1,0:T(8,128)(2,1)S(1)} %convolution_convert_fusion.1, bf16[128,512]{1,0:T(8,128)(2,1)S(1)} %get-tuple-element.40, bf16[128,512]{1,0:T(8,128)(2,1)S(1)} %get-tuple-element.42, ...), kind=kOutput, calls=%fused_computation.2 | convolution fusion | flops 4301258752 | bytes 17301504 | tf_op jit(solution)/shard_map/dot_general | solution.py:63
  342.9 3.6 collective-permute-start.2
  346.5 1.6 collective-permute-start.3
  348.1 3.4 fusion.51
  353.7 3.5 fusion.52
  357.2 10.1 %convert_bitcast_fusion = bf16[32,256,128]{1,2,0:T(8,128)(2,1)} fusion(bf16[32,256,256]{2,1,0:T(8,128)(2,1)} %param.9, f32[32,128,256]{2,1,0:T(8,128)} %fusion.52, f32[32,128,256]{2,1,0:T(8,128)} %fusion.51, bf16[32,256,128]{2,1,0:T(8,128)(2,1)S(1)} %bitcast.100, bf16[32,256,256]{2,1,0:T(8,128)(2,1)} %param.6), kind=kOutput, calls=%fused_computation.13 | convolution fusion | flops 1077936128 | bytes 20971520 | tf_op jit(solution)/shard_map/bij,bjc->bic/dot_general | solution.py:39
  367.3 3.2 copy.12
  370.5 6.4 %fusion.53 = f32[512,128]{1,0:T(8,128)} fusion(bf16[8192,512]{1,0:T(8,128)(2,1)} %copy-done.5, bf16[8192,128]{1,0:T(8,128)(2,1)S(1)} %bitcast.104), kind=kOutput, calls=%fused_computation.101 | convolution fusion | flops 1073741824 | bytes 10747904 | tf_op jit(solution)/shard_map/dot_general | solution.py:21
  376.9 72.2 %all-reduce.6.cloned.1.call-done = f32[512,128]{1,0:T(8,128)} async-done(((f32[512,128]{1,0:T(8,128)}), f32[512,128]{1,0:T(8,128)}) %all-reduce.6.cloned.1.call-update) | async-done | bytes 262160 | tf_op jit(solution)/shard_map/psum | solution.py:66
  449.1 1.7 copy.31
  (67 shorter events, 20.3 us)
Async XLA Ops:
  7.2 95.2 %all-gather.2.cloned.1.call-start = ((), (), s32[]{:S(2)}) async-start(), calls=%async_computation | async-start | bytes 10485760 | tf_op jit(solution)/shard_map/all_gather | solution.py:59
  8.1 13.3 %collective-permute-start.1 = (bf16[256,128]{1,0:T(8,128)(2,1)S(1)}, bf16[256,128]{1,0:T(8,128)(2,1)S(1)}, u32[]{:S(2)}, u32[]{:S(2)}) collective-permute-start(bf16[256,128]{1,0:T(8,128)(2,1)S(1)} %get-tuple-element.26), channel_id=1, source_target_pairs={{4,0},{8,4},{12,8},{16,12},{20,16},{24,20},{28,24},{5,1},{9,5},{13... | collective-permute-start | bytes 196616 | tf_op jit(solution)/shard_map/ppermute | solution.py:15
  9.4 12.0 %collective-permute-start = (bf16[256,128]{1,0:T(8,128)(2,1)S(1)}, bf16[256,128]{1,0:T(8,128)(2,1)S(1)}, u32[]{:S(2)}, u32[]{:S(2)}) collective-permute-start(bf16[256,128]{1,0:T(8,128)(2,1)S(1)} %get-tuple-element.27), channel_id=1, source_target_pairs={{0,4},{4,8},{8,12},{12,16},{16,20},{20,24},{24,28},{1,5},{5,9},{9,... | collective-permute-start | bytes 196616 | tf_op jit(solution)/shard_map/ppermute | solution.py:12
  14.9 6.5 %copy-start.4 = (bf16[8192,128]{1,0:T(8,128)(2,1)S(1)}, bf16[8192,128]{1,0:T(8,128)(2,1)}, u32[]{:S(2)}) copy-start(bf16[8192,128]{1,0:T(8,128)(2,1)} %param.5) | copy-start | bytes 6291460
  21.4 2.2 copy-start.2
  41.2 150.9 %all-reduce.4.cloned.1.call-start = ((), (), s32[]{:S(2)}) async-start(), calls=%async_computation.1 | async-start | bytes 2097152 | tf_op jit(solution)/shard_map/psum | solution.py:60
  113.7 335.5 %all-reduce.6.cloned.1.call-start = ((), (), s32[]{:S(2)}) async-start(), calls=%async_computation.2 | async-start | bytes 524288 | tf_op jit(solution)/shard_map/psum | solution.py:66
  342.5 9.0 %copy-start.5 = (bf16[8192,512]{1,0:T(8,128)(2,1)}, bf16[8192,512]{1,0:T(8,128)(2,1)S(1)}, u32[]{:S(2)}) copy-start(bf16[8192,512]{1,0:T(8,128)(2,1)S(1)} %convolution_convert_fusion) | copy-start | bytes 25165828
  342.5 5.6 %copy-start.3 = (bf16[32,256,256]{2,1,0:T(8,128)(2,1)S(1)}, bf16[32,256,256]{2,1,0:T(8,128)(2,1)}, u32[]{:S(2)}) copy-start(bf16[32,256,256]{2,1,0:T(8,128)(2,1)} %param.7) | copy-start | bytes 12582916
  342.8 9.9 %copy-start = (bf16[8192,128]{1,0:T(8,128)(2,1)}, bf16[8192,128]{1,0:T(8,128)(2,1)S(1)}, u32[]{:S(2)}) copy-start(bf16[8192,128]{1,0:T(8,128)(2,1)S(1)} %constant_dynamic-slice_fusion.2) | copy-start | bytes 6291460
  342.9 8.7 %collective-permute-start.2 = (bf16[256,128]{1,0:T(8,128)(2,1)S(1)}, bf16[256,128]{1,0:T(8,128)(2,1)S(1)}, u32[]{:S(2)}, u32[]{:S(2)}) collective-permute-start(bf16[256,128]{1,0:T(8,128)(2,1)S(1)} %get-tuple-element.20), channel_id=1, source_target_pairs={{0,4},{4,8},{8,12},{12,16},{16,20},{20,24},{24,28},{1,5},{5,9},{9,... | collective-permute-start | bytes 196616 | tf_op jit(solution)/shard_map/ppermute | solution.py:12
  346.5 6.3 %collective-permute-start.3 = (bf16[256,128]{1,0:T(8,128)(2,1)S(1)}, bf16[256,128]{1,0:T(8,128)(2,1)S(1)}, u32[]{:S(2)}, u32[]{:S(2)}) collective-permute-start(bf16[256,128]{1,0:T(8,128)(2,1)S(1)} %get-tuple-element.21), channel_id=1, source_target_pairs={{4,0},{8,4},{12,8},{16,12},{20,16},{24,20},{28,24},{5,1},{9,5},{13... | collective-permute-start | bytes 196616 | tf_op jit(solution)/shard_map/ppermute | solution.py:15
  351.5 2.2 copy-start.1
Sparse Core Ops, SparseCore 0:
  41.3 61.0 all-gather.1
  113.8 78.2 all-reduce.3
  377.1 72.0 all-reduce.5
where the time goes:
time: 465 us; the launch traced here: 458 us
  waiting for transfers between devices  212 us (46%)
  other arithmetic  122 us (26%)
  matrix products  69.1 us (15%)
  local copies, waits for them, and re-layouts  25.2 us (5%)
  between operations  16.9 us (4%)
  starting transfers between devices  12.3 us (3%)
    another operation x14, other arithmetic, inverse_upper(): factor = jnp.linalg.cholesky(gram)  79 us
    psum x1, waiting for transfers between devices, shards(): gram = lax.psum(inner(wide, wide), 'rows')  77.2 us
    psum x1, waiting for transfers between devices, shards(): projected = lax.psum(inner(ortho_all, image), 'rows')  72.2 us
    all_gather x1, waiting for transfers between devices, shards(): wide = lax.all_gather(work, 'cols', axis=1, tiled=True)  61.1 us
    another operation x3, other arithmetic, inverse_upper(): lax.linalg.triangular_solve(factor, identity, left_side=True, lower=True)  40.3 us
    dot_general x2, matrix products, apply_blocks(): jnp.einsum('bij,bjc->bic', inverse, mixed, preferred_element_type=jnp.flo...  20.1 us
    dot_general x2, matrix products, inner(): lax.dot_general(left, right, (((0,), (0,)), ((), ())), preferred_element_...  17.7 us
    another operation x12, local copies, waits for them, and re-layouts  10.8 us
  transfers between devices with their start and end apart: 7, of which 4 were waited for; matrix products, arithmetic and copies ran while one was open for 2% of the time, Pallas kernels for 0%

commit v1 on v0

--- a/solution.py
+++ b/solution.py
@@ -57,7 +57,7 @@
 
     work = operate(basis)
     wide = lax.all_gather(work, "cols", axis=1, tiled=True)
-    gram = lax.psum(inner(wide, wide), "rows")
+    gram = jnp.sum(jax.lax.all_gather(inner(wide, wide), "rows"), axis=0)
     rinv = inverse_upper(gram)
     start = lax.axis_index("cols") * width
     ortho_all = jnp.dot(wide, rinv, preferred_element_type=jnp.float32).astype(jnp.bfloat16)

time: 465 us -> 515 us (1.11)
  waiting for transfers between devices: 212 us -> 258 us
    all_gather x0 -> x1, waiting for transfers between devices: none -> 124 us  [shards(): gram = jnp.sum(jax.lax.all_gather(inner(wide, wide), 'rows'), axis=0)]
    psum x1 -> x0, waiting for transfers between devices: 77.2 us -> none  [shards(): gram = lax.psum(inner(wide, wide), 'rows')]
where the time goes in v1:
time: 515 us; the launch traced here: 509 us
  waiting for transfers between devices  258 us (50%)
  other arithmetic  125 us (24%)
  matrix products  72 us (14%)
  local copies, waits for them, and re-layouts  25.5 us (5%)
  between operations  16.9 us (3%)
  starting transfers between devices  11.7 us (2%)
    all_gather x1, waiting for transfers between devices, shards(): gram = jnp.sum(jax.lax.all_gather(inner(wide, wide), 'rows'), axis=0)  124 us
    another operation x14, other arithmetic, inverse_upper(): factor = jnp.linalg.cholesky(gram)  79.1 us
    psum x1, waiting for transfers between devices, shards(): projected = lax.psum(inner(ortho_all, image), 'rows')  71.7 us
    all_gather x1, waiting for transfers between devices, shards(): wide = lax.all_gather(work, 'cols', axis=1, tiled=True)  61.1 us
    another operation x3, other arithmetic, inverse_upper(): lax.linalg.triangular_solve(factor, identity, left_side=True, lower=True)  40.3 us
    dot_general x2, matrix products, apply_blocks(): jnp.einsum('bij,bjc->bic', inverse, mixed, preferred_element_type=jnp.flo...  20.2 us
    dot_general x2, matrix products, inner(): lax.dot_general(left, right, (((0,), (0,)), ((), ())), preferred_element_...  17.7 us
    another operation x12, local copies, waits for them, and re-layouts  10.5 us
  transfers between devices with their start and end apart: 7, of which 4 were waited for; matrix products, arithmetic and copies ran while one was open for 2% of the time, Pallas kernels for 0%

profile of v1, /device:TPU:0, one launch (start us, length us, event | category | flops | bytes accessed | tf_op | source)
XLA Modules:
  0.0 508.7 jit_solution(17029540484713269794)
XLA Ops:
  9.4 5.5 %collective-permute-start = (bf16[256,128]{1,0:T(8,128)(2,1)S(1)}, bf16[256,128]{1,0:T(8,128)(2,1)S(1)}, u32[]{:S(2)}, u32[]{:S(2)}) collective-permute-start(bf16[256,128]{1,0:T(8,128)(2,1)S(1)} %get-tuple-element.27), channel_id=1, source_target_pairs={{0,4},{4,8},{8,12},{12,16},{16,20},{20,24},{24,28},{1,5},{5,9},{9,... | collective-permute-start | bytes 196616 | tf_op jit(solution)/shard_map/ppermute | solution.py:12
  14.9 6.4 %fusion.49 = f32[32,256,128]{1,2,0:T(8,128)} fusion(bf16[32,256,256]{2,1,0:T(8,128)(2,1)} %param.7, bf16[32,256,128]{2,1,0:T(8,128)(2,1)} %bitcast.99), kind=kOutput, calls=%fused_computation.97 | convolution fusion | flops 536870912 | bytes 10485760 | tf_op jit(solution)/shard_map/bij,bjc->bic/dot_general | solution.py:32
  21.7 1.9 copy-done.2
  23.6 3.5 fusion.48
  27.0 10.1 %convert_bitcast_fusion.1 = bf16[32,256,128]{1,2,0:T(8,128)(2,1)} fusion(bf16[32,256,256]{2,1,0:T(8,128)(2,1)} %param.9, f32[32,256,128]{1,2,0:T(8,128)} %fusion.49, f32[32,128,256]{2,1,0:T(8,128)} %fusion.48, bf16[32,256,128]{2,1,0:T(8,128)(2,1)S(1)} %bitcast.100, bf16[32,256,256]{2,1,0:T(8,128)(2,1)} %param.8), kind=kOutput, calls=%fused_computation.14 | convolution fusion | flops 1077936128 | bytes 20971520 | tf_op jit(solution)/shard_map/bij,bjc->bic/dot_general | solution.py:39
  37.1 4.0 copy.20
  41.2 61.1 %all-gather.4.cloned.1.call-done = bf16[8192,512]{1,0:T(8,128)(2,1)} async-done(((bf16[8192,128]{1,0:T(8,128)(2,1)}), bf16[8192,512]{1,0:T(8,128)(2,1)}) %all-gather.4.cloned.1.call-update) | async-done | bytes 8388624 | tf_op jit(solution)/shard_map/all_gather | solution.py:59
  102.4 11.2 %fusion.50 = f32[512,512]{1,0:T(8,128)} fusion(bf16[8192,512]{1,0:T(8,128)(2,1)} %all-gather.4.cloned.1.call-done), kind=kOutput, calls=%fused_computation.98 | convolution fusion | flops 4294967296 | bytes 9437184 | tf_op jit(solution)/shard_map/dot_general | solution.py:21
  114.1 124.2 %all-gather.6.cloned.1.call-done = f32[4096,512]{1,0:T(8,128)} async-done(((f32[512,512]{1,0:T(8,128)}), f32[4096,512]{1,0:T(8,128)}) %all-gather.6.cloned.1.call-update) | async-done | bytes 8388624 | tf_op jit(solution)/shard_map/all_gather | solution.py:60
  238.3 4.5 reduce_sum.9
  244.3 11.7 %cholesky.104 = f32[128,128]{1,0:T(8,128)S(1)} custom-call(f32[128,128]{1,0:T(8,128)S(1)} %cholesky.266), custom_call_target="Cholesky" | custom-call | tf_op jit(solution)/shard_map/jit(cholesky)/cholesky | solution.py:44
  256.2 9.8 %custom-call.30 = f32[1,128,128]{1,2,0:T(8,128)S(1)} custom-call(f32[1,128,128]{2,1,0:T(8,128)S(1)} %get-tuple-element.37), custom_call_target="InvertDiagBlocksLowerTriangular" | custom-call | tf_op jit(solution)/shard_map/jit(cholesky)/cholesky | solution.py:44
  268.5 11.9 %cholesky.217 = f32[128,128]{1,0:T(8,128)S(1)} custom-call(f32[128,128]{1,0:T(8,128)S(1)} %cholesky.270), custom_call_target="Cholesky" | custom-call | tf_op jit(solution)/shard_map/jit(cholesky)/cholesky | solution.py:44
  280.5 9.8 %custom-call.31 = f32[1,128,128]{1,2,0:T(8,128)S(1)} custom-call(f32[1,128,128]{2,1,0:T(8,128)S(1)} %get-tuple-element.34), custom_call_target="InvertDiagBlocksLowerTriangular" | custom-call | tf_op jit(solution)/shard_map/jit(cholesky)/cholesky | solution.py:44
  291.9 11.7 %cholesky.238 = f32[128,128]{1,0:T(8,128)S(1)} custom-call(f32[128,128]{1,0:T(8,128)S(1)} %cholesky.275), custom_call_target="Cholesky" | custom-call | tf_op jit(solution)/shard_map/jit(cholesky)/cholesky | solution.py:44
  304.3 9.8 %custom-call.32 = f32[1,128,128]{1,2,0:T(8,128)S(1)} custom-call(f32[1,128,128]{2,1,0:T(8,128)S(1)} %get-tuple-element.31), custom_call_target="InvertDiagBlocksLowerTriangular" | custom-call | tf_op jit(solution)/shard_map/jit(cholesky)/cholesky | solution.py:44
  315.6 12.1 %cholesky.255 = f32[128,128]{1,0:T(8,128)S(1)} custom-call(f32[128,128]{1,0:T(8,128)S(1)} %convolution_subtract_fusion.5), custom_call_target="Cholesky" | custom-call | tf_op jit(solution)/shard_map/jit(cholesky)/cholesky | solution.py:44
  331.8 10.6 %while.1 = (s32[]{:T(128)}, f32[512,512]{1,0:T(8,128)S(1)}, s32[4,2]{0,1:T(2,128)S(1)}, f32[4,128,128]{2,1,0:T(8,128)}, s32[]{:T(128)}) while((s32[]{:T(128)}, f32[512,512]{1,0:T(8,128)S(1)}, s32[4,2]{0,1:T(2,128)S(1)}, f32[4,128,128]{2,1,0:T(8,128)}, s32[]{:T(128)}) %tuple.38), condition=%wide.while_cond, body=%wide.while_body.sunk | while | flops 2 | bytes 132205 | solution.py:46
  332.4 2.0 bitcast_dynamic-update-slice_fusion.2
  335.1 2.0 bitcast_dynamic-update-slice_fusion.2
  337.7 2.0 bitcast_dynamic-update-slice_fusion.2
  340.4 2.0 bitcast_dynamic-update-slice_fusion.2
  342.4 40.1 %custom-call.33 = f32[4,128,128]{1,2,0:T(8,128)S(1)} custom-call(f32[4,128,128]{2,1,0:T(8,128)} %get-tuple-element.9), custom_call_target="InvertDiagBlocksLowerTriangular" | custom-call | tf_op jit(solution)/shard_map/triangular_solve | solution.py:46
  385.5 8.8 %convolution_convert_fusion = bf16[8192,512]{1,0:T(8,128)(2,1)S(1)} fusion(bf16[8192,512]{1,0:T(8,128)(2,1)} %all-gather.4.cloned.1.call-done, bf16[128,512]{1,0:T(8,128)(2,1)S(1)} %convolution_convert_fusion.1, bf16[128,512]{1,0:T(8,128)(2,1)S(1)} %get-tuple-element.40, bf16[128,512]{1,0:T(8,128)(2,1)S(1)} %get-tuple-element.42, ...), kind=kOutput, calls=%fused_computation.2 | convolution fusion | flops 4301258752 | bytes 17301504 | tf_op jit(solution)/shard_map/dot_general | solution.py:63
  394.7 2.9 collective-permute-start.2
  397.6 1.7 collective-permute-start.3
  399.7 3.5 fusion.51
  405.4 3.5 fusion.52
  408.8 10.1 %convert_bitcast_fusion = bf16[32,256,128]{1,2,0:T(8,128)(2,1)} fusion(bf16[32,256,256]{2,1,0:T(8,128)(2,1)} %param.9, f32[32,128,256]{2,1,0:T(8,128)} %fusion.52, f32[32,128,256]{2,1,0:T(8,128)} %fusion.51, bf16[32,256,128]{2,1,0:T(8,128)(2,1)S(1)} %bitcast.101, bf16[32,256,256]{2,1,0:T(8,128)(2,1)} %param.6), kind=kOutput, calls=%fused_computation.13 | convolution fusion | flops 1077936128 | bytes 20971520 | tf_op jit(solution)/shard_map/bij,bjc->bic/dot_general | solution.py:39
  418.9 3.2 copy.25
  422.1 6.4 %fusion.53 = f32[512,128]{1,0:T(8,128)} fusion(bf16[8192,512]{1,0:T(8,128)(2,1)} %copy-done.6, bf16[8192,128]{1,0:T(8,128)(2,1)S(1)} %bitcast.106), kind=kOutput, calls=%fused_computation.101 | convolution fusion | flops 1073741824 | bytes 10747904 | tf_op jit(solution)/shard_map/dot_general | solution.py:21
  428.6 71.7 %all-reduce.3.cloned.1.call-done = f32[512,128]{1,0:T(8,128)} async-done(((f32[512,128]{1,0:T(8,128)}), f32[512,128]{1,0:T(8,128)}) %all-reduce.3.cloned.1.call-update) | async-done | bytes 262160 | tf_op jit(solution)/shard_map/psum | solution.py:66
  (70 shorter events, 22.6 us)
Async XLA Ops:
  7.2 95.2 %all-gather.4.cloned.1.call-start = ((), (), s32[]{:S(2)}) async-start(), calls=%async_computation | async-start | bytes 10485760 | tf_op jit(solution)/shard_map/all_gather | solution.py:59
  8.1 13.3 %collective-permute-start.1 = (bf16[256,128]{1,0:T(8,128)(2,1)S(1)}, bf16[256,128]{1,0:T(8,128)(2,1)S(1)}, u32[]{:S(2)}, u32[]{:S(2)}) collective-permute-start(bf16[256,128]{1,0:T(8,128)(2,1)S(1)} %get-tuple-element.26), channel_id=1, source_target_pairs={{4,0},{8,4},{12,8},{16,12},{20,16},{24,20},{28,24},{5,1},{9,5},{13... | collective-permute-start | bytes 196616 | tf_op jit(solution)/shard_map/ppermute | solution.py:15
  9.4 12.0 %collective-permute-start = (bf16[256,128]{1,0:T(8,128)(2,1)S(1)}, bf16[256,128]{1,0:T(8,128)(2,1)S(1)}, u32[]{:S(2)}, u32[]{:S(2)}) collective-permute-start(bf16[256,128]{1,0:T(8,128)(2,1)S(1)} %get-tuple-element.27), channel_id=1, source_target_pairs={{0,4},{4,8},{8,12},{12,16},{16,20},{20,24},{24,28},{1,5},{5,9},{9,... | collective-permute-start | bytes 196616 | tf_op jit(solution)/shard_map/ppermute | solution.py:12
  14.9 6.5 %copy-start.4 = (bf16[8192,128]{1,0:T(8,128)(2,1)S(1)}, bf16[8192,128]{1,0:T(8,128)(2,1)}, u32[]{:S(2)}) copy-start(bf16[8192,128]{1,0:T(8,128)(2,1)} %param.5) | copy-start | bytes 6291460
  21.4 2.2 copy-start.2
  41.2 197.1 %all-gather.6.cloned.1.call-start = ((), (), s32[]{:S(2)}) async-start(), calls=%async_computation.2 | async-start | bytes 9437184 | tf_op jit(solution)/shard_map/all_gather | solution.py:60
  113.6 386.7 %all-reduce.3.cloned.1.call-start = ((), (), s32[]{:S(2)}) async-start(), calls=%async_computation.1 | async-start | bytes 524288 | tf_op jit(solution)/shard_map/psum | solution.py:66
  243.3 1.0 copy-start.5
  394.4 8.8 %copy-start.6 = (bf16[8192,512]{1,0:T(8,128)(2,1)}, bf16[8192,512]{1,0:T(8,128)(2,1)S(1)}, u32[]{:S(2)}) copy-start(bf16[8192,512]{1,0:T(8,128)(2,1)S(1)} %convolution_convert_fusion) | copy-start | bytes 25165828
  394.4 5.3 %copy-start.3 = (bf16[32,256,256]{2,1,0:T(8,128)(2,1)S(1)}, bf16[32,256,256]{2,1,0:T(8,128)(2,1)}, u32[]{:S(2)}) copy-start(bf16[32,256,256]{2,1,0:T(8,128)(2,1)} %param.7) | copy-start | bytes 12582916
  394.7 9.3 %copy-start = (bf16[8192,128]{1,0:T(8,128)(2,1)}, bf16[8192,128]{1,0:T(8,128)(2,1)S(1)}, u32[]{:S(2)}) copy-start(bf16[8192,128]{1,0:T(8,128)(2,1)S(1)} %constant_dynamic-slice_fusion.2) | copy-start | bytes 6291460
  394.7 8.5 %collective-permute-start.2 = (bf16[256,128]{1,0:T(8,128)(2,1)S(1)}, bf16[256,128]{1,0:T(8,128)(2,1)S(1)}, u32[]{:S(2)}, u32[]{:S(2)}) collective-permute-start(bf16[256,128]{1,0:T(8,128)(2,1)S(1)} %get-tuple-element.20), channel_id=1, source_target_pairs={{0,4},{4,8},{8,12},{12,16},{16,20},{20,24},{24,28},{1,5},{5,9},{9,... | collective-permute-start | bytes 196616 | tf_op jit(solution)/shard_map/ppermute | solution.py:12
  397.6 6.4 %collective-permute-start.3 = (bf16[256,128]{1,0:T(8,128)(2,1)S(1)}, bf16[256,128]{1,0:T(8,128)(2,1)S(1)}, u32[]{:S(2)}, u32[]{:S(2)}) collective-permute-start(bf16[256,128]{1,0:T(8,128)(2,1)S(1)} %get-tuple-element.21), channel_id=1, source_target_pairs={{4,0},{8,4},{12,8},{16,12},{20,16},{24,20},{28,24},{5,1},{9,5},{13... | collective-permute-start | bytes 196616 | tf_op jit(solution)/shard_map/ppermute | solution.py:15
  403.2 2.2 copy-start.1
Sparse Core Ops, SparseCore 0:
  41.3 61.0 all-gather.3
  113.8 124.4 all-gather.5
  428.7 71.5 all-reduce.2
